TPU v7x, 32 devices: a whole 2x2x4 slice. The times are simulated.
32 devices in a mesh: rows: 8 (over z, y), feat: 4 (over x, core).
Axes of the slice: x: 2, y: 2, z: 4, core: 2. Of those that a mesh axis runs over, the one named last changes fastest.
Arguments:
- cells: bfloat16 [1024, 80, 128], P('rows', 'feat'), may hold values from -19 to 19
- block_table: int32 [8], replicated, may hold values from 0 to 7, as said below
- row_live: int32 [1024], replicated, may hold values from 0 to 1, as said below
- row_train: int32 [1024], replicated, may hold values from 0 to 1, as said below
- feat_qkv: bfloat16 [128, 384], replicated, may hold values from -0.5 to 0.5
- feat_out: bfloat16 [128, 128], replicated, may hold values from -0.5 to 0.5
- item_qkv: bfloat16 [128, 384], replicated, may hold values from -0.5 to 0.5
- item_out: bfloat16 [128, 128], replicated, may hold values from -0.5 to 0.5
Outputs:
- layer_output: bfloat16 [1024, 80, 128], P(('rows', 'feat'))
Inputs may be any that keep to these rules, and one draw needn't show every extreme that they name: `block_table`: every table number appears in some block. `row_live`: every training row is live. `row_train`: each aligned group of 32 rows holds 1 to 4 training rows; some group holds exactly 4.
All inputs are finite; a program needn't handle non-finite values.
Results may differ from a plain program's by a relative error of at most 0.014.
Values may be sent and summed in bfloat16 or wider, within the bound.
No kernel may reach another device: no remote copies, remote signals or barrier semaphores. Data moves between devices by JAX's collectives and lax.ppermute only.
A program may use at most 64 MiB of HBM per device.

v0:
```python
import jax
import jax.numpy as jnp
from jax import lax
from jax.sharding import PartitionSpec as P

HEADS = 4
HEAD_DIM = 32
KEEP = 4
TABLES = 8
EPSILON = 1e-05
MASKED = -1e30


def compact_train(train_rows):
    positions = jnp.arange(train_rows.shape[-1], dtype=jnp.int32)
    ordinal = jnp.cumsum(train_rows, axis=-1) - 1
    slot_ids = jnp.arange(KEEP, dtype=jnp.int32)
    matched = (train_rows[..., None, :] == 1) & (ordinal[..., None, :] == slot_ids[:, None])
    return jnp.sum(jnp.where(matched, positions, 0), axis=-1)


def into_heads(tensor):
    return tensor.reshape(tensor.shape[:-1] + (HEADS, HEAD_DIM))


def attend_features(queries, key_part, value_part):
    row_count, query_feats = (queries.shape[0], queries.shape[1])
    blocks = max(1, row_count * query_feats // 1280)
    while row_count % blocks:
        blocks -= 1
    scaling = HEAD_DIM ** (-0.5)

    def attend_one_block(block_parts):
        block_query, block_key, block_value = block_parts
        scores = (
            jnp.einsum(
                "rqhd,rkhd->rhqk", block_query, block_key, preferred_element_type=jnp.float32
            )
            * scaling
        )
        shares = jax.nn.softmax(scores, axis=-1).astype(jnp.bfloat16)
        return jnp.einsum(
            "rhqk,rkhd->rqhd", shares, block_value, preferred_element_type=jnp.float32
        ).astype(jnp.bfloat16)

    def by_block(tensor):
        return tensor.reshape((blocks, row_count // blocks) + tensor.shape[1:])

    result = lax.map(
        attend_one_block, (by_block(queries), by_block(key_part), by_block(value_part))
    )
    return result.reshape(row_count, query_feats, HEADS * HEAD_DIM)


def feature_layer(normed_cells, feat_out, key_part, value_part, queries):
    attended = attend_features(queries, key_part, value_part)
    update = jnp.dot(attended, feat_out, preferred_element_type=jnp.float32)
    return (normed_cells.astype(jnp.float32) + update).astype(jnp.bfloat16)


def on_device(cells, block_table, row_live, row_train, feat_qkv, feat_out, item_qkv, item_out):
    rows_here, feats_here, width_all = cells.shape
    row_index = lax.axis_index("rows")
    feat_index = lax.axis_index("feat")
    row_devices = lax.axis_size("rows")
    feat_devices = lax.axis_size("feat")
    my_table = lax.dynamic_index_in_dim(block_table, row_index, keepdims=False)
    live_rows = lax.dynamic_slice_in_dim(row_live, row_index * rows_here, rows_here).astype(
        jnp.float32
    )
    values = cells.astype(jnp.float32)
    table_hot = (jnp.arange(TABLES, dtype=jnp.int32) == my_table).astype(jnp.float32)
    first_local = jnp.sum(values * live_rows[:, None, None], axis=(0, 2))
    count_local = jnp.sum(live_rows) * width_all
    first_sum, count_sum = lax.psum(
        (table_hot[:, None] * first_local[None, :], table_hot * count_local), "rows"
    )
    table_mean = first_sum / count_sum[:, None]
    mine_mean = lax.dynamic_index_in_dim(table_mean, my_table, keepdims=False)
    centred = values - mine_mean[None, :, None]
    second_local = jnp.sum(centred * centred * live_rows[:, None, None], axis=(0, 2))
    second_sum = lax.psum(table_hot[:, None] * second_local[None, :], "rows")
    table_spread = second_sum / count_sum[:, None]
    mine_spread = lax.dynamic_index_in_dim(table_spread, my_table, keepdims=False)
    normed = (centred * lax.rsqrt(mine_spread + EPSILON)[None, :, None]).astype(jnp.bfloat16)
    normed_rows = lax.all_to_all(normed, "feat", split_axis=0, concat_axis=1, tiled=True)
    projected = jnp.dot(normed_rows, feat_qkv, preferred_element_type=jnp.float32).astype(
        jnp.bfloat16
    )
    queries = into_heads(projected[..., :width_all])
    key_part = into_heads(projected[..., width_all : 2 * width_all])
    value_part = into_heads(projected[..., 2 * width_all :])
    mixed_rows = feature_layer(normed_rows, feat_out, key_part, value_part, queries)
    group_rows, total_feats = (mixed_rows.shape[0], mixed_rows.shape[1])
    per_device = total_feats * HEADS // row_devices
    first_row = row_index * rows_here + feat_index * group_rows
    train_here = lax.dynamic_slice_in_dim(row_train, first_row, group_rows)
    places = compact_train(train_here)
    chosen = jnp.take(mixed_rows, places, axis=0)
    item_query = jnp.dot(
        mixed_rows, item_qkv[:, :width_all], preferred_element_type=jnp.float32
    ).astype(jnp.bfloat16)
    item_query = item_query.reshape(group_rows, row_devices, per_device, HEAD_DIM)
    key_value = jnp.dot(chosen, item_qkv[:, width_all:], preferred_element_type=jnp.float32).astype(
        jnp.bfloat16
    )
    item_key = key_value[..., :width_all].reshape(KEEP, row_devices, per_device, HEAD_DIM)
    item_value = key_value[..., width_all:].reshape(KEEP, row_devices, per_device, HEAD_DIM)
    query_table = jnp.repeat(block_table, group_rows)
    groups_all = row_train.reshape(row_devices, feat_devices, group_rows)
    group_counts = jnp.sum(groups_all, axis=2)
    slot_ids = jnp.arange(KEEP, dtype=jnp.int32)
    key_valid = slot_ids[None, None, :] < jnp.transpose(group_counts)[:, :, None]
    key_table = jnp.broadcast_to(block_table[None, :, None], key_valid.shape)
    allowed = (query_table[:, None] == key_table.reshape(-1)[None, :]) & key_valid.reshape(-1)[
        None, :
    ]
    query_count = query_table.shape[0]
    key_count = allowed.shape[1]
    query_blocks = max(1, query_count // 512)
    while query_count % query_blocks:
        query_blocks -= 1
    scaling = HEAD_DIM ** (-0.5)
    blocked_allowed = allowed.reshape(query_blocks, query_count // query_blocks, key_count)
    local_query = lax.all_to_all(item_query, "rows", split_axis=1, concat_axis=0, tiled=True)
    local_key = lax.all_to_all(item_key, "rows", split_axis=1, concat_axis=0, tiled=True)
    local_value = lax.all_to_all(item_value, "rows", split_axis=1, concat_axis=0, tiled=True)
    every_key = lax.all_gather(local_key, "feat", axis=0, tiled=True)
    every_value = lax.all_gather(local_value, "feat", axis=0, tiled=True)

    def one_item(item_parts):
        single_query, single_key, single_value = item_parts

        def one_one_block(block_parts):
            block_query, block_allowed = block_parts
            scores = (
                jnp.dot(block_query, single_key.T, preferred_element_type=jnp.float32) * scaling
            )
            scores = jnp.where(block_allowed, scores, MASKED)
            shares = jax.nn.softmax(scores, axis=-1).astype(jnp.bfloat16)
            return jnp.dot(shares, single_value, preferred_element_type=jnp.float32).astype(
                jnp.bfloat16
            )

        blocked_query = single_query.reshape(query_blocks, query_count // query_blocks, HEAD_DIM)
        return lax.map(one_one_block, (blocked_query, blocked_allowed)).reshape(
            query_count, HEAD_DIM
        )

    by_item = (
        jnp.moveaxis(local_query[:, 0], 1, 0),
        jnp.moveaxis(every_key[:, 0], 1, 0),
        jnp.moveaxis(every_value[:, 0], 1, 0),
    )
    result = jnp.moveaxis(lax.map(one_item, by_item), 0, 1)[:, None]
    attended = lax.all_to_all(result, "rows", split_axis=0, concat_axis=1, tiled=True)
    attended = attended.reshape(group_rows, total_feats, width_all)
    update = jnp.dot(attended, item_out, preferred_element_type=jnp.float32)
    return (mixed_rows.astype(jnp.float32) + update).astype(jnp.bfloat16)


def solution(mesh):
    return jax.shard_map(
        on_device,
        mesh=mesh,
        in_specs=(P("rows", "feat", None), P(), P(), P(), P(), P(), P(), P()),
        out_specs=P(("rows", "feat"), None, None),
        check_vma=False,
    )
```

profile of v0, /device:TPU:0, one launch (start us, length us, event | category | flops | bytes accessed | tf_op | source)
XLA Modules:
  0.0 317.5 jit_solution(12919230653871559837)
XLA Ops:
  5.5 1.6 fusion.40
  7.2 23.4 %all-reduce = (f32[8,20]{1,0:T(8,128)S(1)}, f32[8]{0:T(128)S(1)}) all-reduce(f32[8,20]{1,0:T(8,128)S(1)} %broadcast_multiply_fusion.1, f32[8]{0:T(128)S(1)} %compare_select_fusion.2), channel_id=1, replica_groups=mesh['rows'=8,'feat'=4] {'rows'}, use_global_device_ids=true, to_apply=%region_1.2 | all-reduce | flops 168 | bytes 1344 | tf_op jit(solution)/shard_map/psum | solution.py:75
  31.2 1.7 fusion.38
  33.0 17.1 %psum.23 = f32[8,20]{1,0:T(8,128)S(1)} all-reduce(f32[8,20]{1,0:T(8,128)S(1)} %broadcast_multiply_fusion), channel_id=1, replica_groups=mesh['rows'=8,'feat'=4] {'rows'}, use_global_device_ids=true, to_apply=%region_5.6 | all-reduce | flops 160 | bytes 1280 | tf_op jit(solution)/shard_map/psum | solution.py:82
  50.2 2.5 fusion.39
  52.6 3.5 %all-to-all-start = ((bf16[128,20,128]{2,1,0:T(8,128)(2,1)}), bf16[128,20,128]{2,1,0:T(8,128)(2,1)S(1)}, u32[]{:S(2)}, u32[]{:S(2)}) async-start(bf16[128,20,128]{2,1,0:T(8,128)(2,1)} %fusion.39), calls=%async_computation | async-start | bytes 1572864 | tf_op jit(solution)/shard_map/all_to_all | solution.py:86
  56.7 11.0 %all-to-all-done = bf16[128,20,128]{2,1,0:T(8,128)(2,1)S(1)} async-done(((bf16[128,20,128]{2,1,0:T(8,128)(2,1)}), bf16[128,20,128]{2,1,0:T(8,128)(2,1)S(1)}, u32[]{:S(2)}, u32[]{:S(2)}) %all-to-all-start) | async-done | bytes 655392 | tf_op jit(solution)/shard_map/all_to_all | solution.py:86
  72.3 11.1 %while.25 = (s32[]{:T(128)}, bf16[2,16,80,4,32]{2,4,3,1,0:T(8,128)(2,1)}, bf16[2,16,80,4,32]{2,4,3,1,0:T(8,128)(2,1)}, bf16[2,16,80,4,32]{2,4,3,1,0:T(8,128)(2,1...) while((s32[]{:T(128)}, bf16[2,16,80,4,32]{2,4,3,1,0:T(8,128)(2,1)}, ...), condition=%wide.region_9.10_spmd, body=%wide.region_6.9_spmd.sunk | while | flops 55050320 | bytes 17553560 | solution.py:49
  72.9 3.4 %fusion.79 = (f32[16,4,80]{2,1,0:T(4,128)S(1)}, f32[16,4,80,80]{2,3,1,0:T(8,128)S(1)}) fusion(f32[16,4,80,80]{2,3,1,0:T(8,128)S(1)} %fusion.78), kind=kOutput, calls=%fused_computation.89.clone.1 | output fusion | flops 1638479 | bytes 3297280 | tf_op jit(solution)/shard_map/while/body/eval_jaxpr/sub | solution.py:41
  78.5 3.4 %fusion.79 = (f32[16,4,80]{2,1,0:T(4,128)S(1)}, f32[16,4,80,80]{2,3,1,0:T(8,128)S(1)}) fusion(f32[16,4,80,80]{2,3,1,0:T(8,128)S(1)} %fusion.78), kind=kOutput, calls=%fused_computation.89.clone.1 | output fusion | flops 1638479 | bytes 3297280 | tf_op jit(solution)/shard_map/while/body/eval_jaxpr/sub | solution.py:41
  83.4 1.9 fusion.41
  87.6 3.4 %all-to-all-start.2 = ((bf16[8,2,2560]{2,1,0:T(2,128)(2,1)}), bf16[8,2,2560]{2,1,0:T(2,128)(2,1)S(1)}, u32[]{:S(2)}, u32[]{:S(2)}) async-start(bf16[8,2,2560]{2,1,0:T(2,128)(2,1)} %reshape.214), calls=%async_computation.2 | async-start | bytes 163840 | tf_op jit(solution)/shard_map/all_to_all | solution.py:126
  92.3 5.6 %all-to-all-done.2 = bf16[8,2,2560]{2,1,0:T(2,128)(2,1)S(1)} async-done(((bf16[8,2,2560]{2,1,0:T(2,128)(2,1)}), bf16[8,2,2560]{2,1,0:T(2,128)(2,1)S(1)}, u32[]{:S(2)}, u32[]{:S(2)}) %all-to-all-start.2) | async-done | bytes 81952 | tf_op jit(solution)/shard_map/all_to_all | solution.py:126
  97.9 3.4 %all-to-all-start.3 = ((bf16[8,2,2560]{2,1,0:T(2,128)(2,1)}), bf16[8,2,2560]{2,1,0:T(2,128)(2,1)S(1)}, u32[]{:S(2)}, u32[]{:S(2)}) async-start(bf16[8,2,2560]{2,1,0:T(2,128)(2,1)} %reshape.216), calls=%async_computation.3 | async-start | bytes 163840 | tf_op jit(solution)/shard_map/all_to_all | solution.py:127
  102.4 3.1 reshape.193
  105.5 2.5 copy.118
  107.9 5.7 %reshape.212 = bf16[8,2,20480]{2,1,0:T(2,128)(2,1)} reshape(bf16[8,32,32,40]{3,2,1,0:T(8,128)(2,1)} %bitcast.134) | data formatting | bytes 1310720
  113.7 5.9 %all-to-all-start.1 = ((bf16[8,2,20480]{2,1,0:T(2,128)(2,1)}), bf16[8,2,20480]{2,1,0:T(2,128)(2,1)}, u32[]{:S(2)}, u32[]{:S(2)}) async-start(bf16[8,2,20480]{2,1,0:T(2,128)(2,1)} %reshape.212), calls=%async_computation.1 | async-start | bytes 1310720 | tf_op jit(solution)/shard_map/all_to_all | solution.py:125
  120.9 9.1 %all_gather.6 = bf16[128,1,40,32]{2,3,1,0:T(8,128)(2,1)S(1)} all-gather(bf16[32,1,40,32]{2,3,1,0:T(8,128)(2,1)S(1)} %bitcast.143), channel_id=1, replica_groups=mesh['rows'=8,'feat'=4] {'feat'}, dimensions={0}, use_global_device_ids=true | all-gather | bytes 409600 | tf_op jit(solution)/shard_map/all_gather | solution.py:128
  130.0 2.9 copy.125
  133.3 10.2 %all_gather.7 = bf16[128,1,40,32]{2,3,1,0:T(8,128)(2,1)S(1)} all-gather(bf16[32,1,40,32]{2,3,1,0:T(8,128)(2,1)S(1)} %bitcast.144), channel_id=1, replica_groups=mesh['rows'=8,'feat'=4] {'feat'}, dimensions={0}, use_global_device_ids=true | all-gather | bytes 409600 | tf_op jit(solution)/shard_map/all_gather | solution.py:129
  143.5 2.9 copy.126
  146.3 5.0 %reshape.213 = bf16[8,32,32,40]{3,2,1,0:T(8,128)(2,1)S(1)} reshape(bf16[8,2,20480]{2,1,0:T(2,128)(2,1)} %all-to-all-done.1) | data formatting | bytes 1310720
  151.4 4.9 %copy.124 = bf16[40,256,32]{2,1,0:T(8,128)(2,1)} copy(bf16[40,256,32]{0,2,1:T(8,128)(2,1)S(1)} %bitcast.135) | data formatting | bytes 1310720
  156.3 105.4 %while.26 = (s32[]{:T(128)}, bf16[40,256,32]{1,2,0:T(8,128)(2,1)}, bf16[40,256,32]{2,1,0:T(8,128)(2,1)}, bf16[40,128,32]{2,1,0:T(8,128)(2,1)}, bf16[40,128,32]{2...) while((s32[]{:T(128)}, bf16[40,256,32]{1,2,0:T(8,128)(2,1)}, ...), condition=%wide.region_16.17_spmd.clone, body=%wide.region_13.16_spmd.clone.sunk | while | flops 4529666 | bytes 549597 | solution.py:155
  157.4 1.6 fusion.84
  160.0 1.6 fusion.84
  162.6 1.6 fusion.84
  165.3 1.6 fusion.84
  167.9 1.6 fusion.84
  170.5 1.6 fusion.84
  173.2 1.6 fusion.84
  175.8 1.6 fusion.84
  178.4 1.6 fusion.84
  181.1 1.6 fusion.84
  183.7 1.6 fusion.84
  186.4 1.6 fusion.84
  210.1 1.6 fusion.84
  215.3 1.6 fusion.84
  260.2 1.6 fusion.84
  261.7 4.5 %copy.127 = bf16[40,256,32]{0,2,1:T(8,128)(2,1)S(1)} copy(bf16[40,256,32]{1,2,0:T(8,128)(2,1)} %get-tuple-element.83) | data formatting | bytes 1310720 | tf_op jit(solution)/shard_map/while | solution.py:155
  266.2 1.7 bitcast_bitcast_fusion
  267.9 5.0 %reshape.218 = bf16[8,2,20480]{2,1,0:T(2,128)(2,1)S(1)} reshape(bf16[256,1,32,40]{3,2,1,0:T(8,128)(2,1)} %bitcast_bitcast_fusion) | data formatting | bytes 1310720
  273.0 24.0 %all_to_all.84 = bf16[8,2,20480]{2,1,0:T(2,128)(2,1)S(1)} all-to-all(bf16[8,2,20480]{2,1,0:T(2,128)(2,1)S(1)} %reshape.218), channel_id=1, replica_groups=mesh['rows'=8,'feat'=4] {'rows'}, dimensions={0} | all-to-all | bytes 1310720 | tf_op jit(solution)/shard_map/all_to_all | solution.py:156
  297.0 4.3 %reshape.219 = bf16[256,1,32,40]{3,2,1,0:T(8,128)(2,1)} reshape(bf16[8,2,20480]{2,1,0:T(2,128)(2,1)S(1)} %all_to_all.84) | data formatting | bytes 1310720
  301.3 5.9 %copy.135 = bf16[8,32,1,40,32]{1,0,4,3,2:T(8,128)(2,1)S(1)} copy(bf16[8,32,1,40,32]{3,4,1,0,2:T(8,128)(2,1)} %bitcast.136) | data formatting | bytes 1310720 | tf_op jit(solution)/shard_map/all_to_all | solution.py:156
  307.2 5.6 %copy.129 = bf16[32,8,1,40,32]{4,3,1,0,2:T(8,128)(2,1)} copy(bf16[32,8,1,40,32]{0,1,4,3,2:T(8,128)(2,1)S(1)} %bitcast.133) | data formatting | bytes 1310720 | tf_op jit(solution)/shard_map/all_to_all | solution.py:156
  312.8 3.6 %reshape.197 = bf16[32,80,128]{2,1,0:T(8,128)(2,1)S(1)} reshape(bf16[32,8,1,40,32]{4,3,1,0,2:T(8,128)(2,1)} %copy.129) | data formatting | bytes 1310720 | tf_op jit(solution)/shard_map/reshape | solution.py:157
  (186 shorter events, 102.8 us)
Async XLA Ops:
  0.0 68.7 %copy-start = (bf16[128,384]{1,0:T(8,128)(2,1)S(1)}, bf16[128,384]{1,0:T(8,128)(2,1)}, u32[]{:S(2)}) copy-start(bf16[128,384]{1,0:T(8,128)(2,1)} %param.16) | copy-start | bytes 294916
  7.1 49.0 %copy-start.8 = (s32[1024]{0:T(1024)S(1)}, s32[1024]{0:T(1024)}, u32[]{:S(2)}) copy-start(s32[1024]{0:T(1024)} %param.15) | copy-start | bytes 12292
  52.6 15.1 %all-to-all-start = ((bf16[128,20,128]{2,1,0:T(8,128)(2,1)}), bf16[128,20,128]{2,1,0:T(8,128)(2,1)S(1)}, u32[]{:S(2)}, u32[]{:S(2)}) async-start(bf16[128,20,128]{2,1,0:T(8,128)(2,1)} %fusion.39), calls=%async_computation | async-start | bytes 1572864 | tf_op jit(solution)/shard_map/all_to_all | solution.py:86
  67.9 0.8 copy-start.1
  72.3 11.1 %copy-start.6 = (bf16[128,128]{1,0:T(8,128)(2,1)S(1)}, bf16[128,128]{1,0:T(8,128)(2,1)}, u32[]{:S(2)}) copy-start(bf16[128,128]{1,0:T(8,128)(2,1)} %param.17) | copy-start | bytes 98308
  72.9 3.5 %copy-start.2 = (bf16[2,16,80,4,32]{2,4,3,1,0:T(8,128)(2,1)S(1)}, bf16[2,16,80,4,32]{2,4,3,1,0:T(8,128)(2,1)}, u32[]{:S(2)}) copy-start(bf16[2,16,80,4,32]{2,4,3,1,0:T(8,128)(2,1)} %get-tuple-element.284) | copy-start | bytes 1966084 | tf_op jit(solution)/shard_map/while
  72.9 3.5 %copy-start.4 = (bf16[2,16,80,4,32]{2,4,3,1,0:T(8,128)(2,1)S(1)}, bf16[2,16,80,4,32]{2,4,3,1,0:T(8,128)(2,1)}, u32[]{:S(2)}) copy-start(bf16[2,16,80,4,32]{2,4,3,1,0:T(8,128)(2,1)} %get-tuple-element.291) | copy-start | bytes 1966084 | tf_op jit(solution)/shard_map/while
  76.9 1.0 copy-start.3
  78.4 3.5 %copy-start.2 = (bf16[2,16,80,4,32]{2,4,3,1,0:T(8,128)(2,1)S(1)}, bf16[2,16,80,4,32]{2,4,3,1,0:T(8,128)(2,1)}, u32[]{:S(2)}) copy-start(bf16[2,16,80,4,32]{2,4,3,1,0:T(8,128)(2,1)} %get-tuple-element.284) | copy-start | bytes 1966084 | tf_op jit(solution)/shard_map/while
  78.4 3.5 %copy-start.4 = (bf16[2,16,80,4,32]{2,4,3,1,0:T(8,128)(2,1)S(1)}, bf16[2,16,80,4,32]{2,4,3,1,0:T(8,128)(2,1)}, u32[]{:S(2)}) copy-start(bf16[2,16,80,4,32]{2,4,3,1,0:T(8,128)(2,1)} %get-tuple-element.291) | copy-start | bytes 1966084 | tf_op jit(solution)/shard_map/while
  82.4 1.0 copy-start.3
  83.4 2.5 copy-start.5
  87.6 10.3 %all-to-all-start.2 = ((bf16[8,2,2560]{2,1,0:T(2,128)(2,1)}), bf16[8,2,2560]{2,1,0:T(2,128)(2,1)S(1)}, u32[]{:S(2)}, u32[]{:S(2)}) async-start(bf16[8,2,2560]{2,1,0:T(2,128)(2,1)} %reshape.214), calls=%async_computation.2 | async-start | bytes 163840 | tf_op jit(solution)/shard_map/all_to_all | solution.py:126
  97.9 15.8 %all-to-all-start.3 = ((bf16[8,2,2560]{2,1,0:T(2,128)(2,1)}), bf16[8,2,2560]{2,1,0:T(2,128)(2,1)S(1)}, u32[]{:S(2)}, u32[]{:S(2)}) async-start(bf16[8,2,2560]{2,1,0:T(2,128)(2,1)} %reshape.216), calls=%async_computation.3 | async-start | bytes 163840 | tf_op jit(solution)/shard_map/all_to_all | solution.py:127
  107.9 12.2 %copy-start.9 = (s32[8]{0:T(128)S(1)}, s32[8]{0:T(128)}, u32[]{:S(2)}) copy-start(s32[8]{0:T(128)} %param.13) | copy-start | bytes 100
  113.7 32.7 %all-to-all-start.1 = ((bf16[8,2,20480]{2,1,0:T(2,128)(2,1)}), bf16[8,2,20480]{2,1,0:T(2,128)(2,1)}, u32[]{:S(2)}, u32[]{:S(2)}) async-start(bf16[8,2,20480]{2,1,0:T(2,128)(2,1)} %reshape.212), calls=%async_computation.1 | async-start | bytes 1310720 | tf_op jit(solution)/shard_map/all_to_all | solution.py:125
  312.8 3.6 %copy-start.7 = (bf16[128,128]{1,0:T(8,128)(2,1)S(1)}, bf16[128,128]{1,0:T(8,128)(2,1)}, u32[]{:S(2)}) copy-start(bf16[128,128]{1,0:T(8,128)(2,1)} %param.19) | copy-start | bytes 98308
where the time goes:
time: 323 us; the launch traced here: 318 us
  matrix products  111 us (34%)
  blocking collectives  83.7 us (26%)
  local copies, waits for them, and re-layouts  69.6 us (22%)
  other arithmetic  18 us (6%)
  waiting for transfers between devices  16.6 us (5%)
  starting transfers between devices  16.1 us (5%)
    dot_general x40, matrix products, one_one_block(): jnp.dot(shares, single_value, preferred_element_type=jnp.float32)  62.3 us
    dot_general x40, matrix products, one_one_block(): jnp.dot(block_query, single_key.T, preferred_element_type=jnp.float32)  41.1 us
    unnamed x27, local copies, waits for them, and re-layouts  36.2 us
    all_to_all x1, blocking collectives, on_device(): lax.all_to_all(result, 'rows', split_axis=0, concat_axis=1, tiled=True)  24 us
    psum x1, blocking collectives, on_device(): lax.psum((table_hot[:, None] * first_local[None, :], table_hot * count_lo...  23.4 us
    psum x1, blocking collectives, on_device(): second_sum = lax.psum(table_hot[:, None] * second_local[None, :], 'rows')  17.1 us
    all_to_all x2, local copies, waits for them, and re-layouts, on_device(): lax.all_to_all(result, 'rows', split_axis=0, concat_axis=1, tiled=True)  11.5 us
    all_to_all x1, waiting for transfers between devices, on_device(): lax.all_to_all(normed, 'feat', split_axis=0, concat_axis=1, tiled=True)  11 us
  transfers between devices with their start and end apart: 4, of which 2 were waited for; matrix products, arithmetic and copies ran while one was open for 7% of the time, Pallas kernels for 0%

commit v1 on v0

--- a/solution.py
+++ b/solution.py
@@ -9,6 +9,12 @@
 TABLES = 8
 EPSILON = 1e-05
 MASKED = -1e30
+
+
+def trade_parts(x, mesh_axis, split, join):
+    cells = jnp.split(x, lax.axis_size(mesh_axis), axis=split)
+    received = lax.all_to_all(jnp.stack(cells), mesh_axis, 0, 0)
+    return jnp.concatenate(received, axis=join)
 
 
 def compact_train(train_rows):
@@ -153,7 +159,7 @@
         jnp.moveaxis(every_value[:, 0], 1, 0),
     )
     result = jnp.moveaxis(lax.map(one_item, by_item), 0, 1)[:, None]
-    attended = lax.all_to_all(result, "rows", split_axis=0, concat_axis=1, tiled=True)
+    attended = trade_parts(result, "rows", 0, 1)
     attended = attended.reshape(group_rows, total_feats, width_all)
     update = jnp.dot(attended, item_out, preferred_element_type=jnp.float32)
     return (mixed_rows.astype(jnp.float32) + update).astype(jnp.bfloat16)

time: 323 us -> 288 us (0.89)
  matrix products: 111 us -> 89.1 us
  local copies, waits for them, and re-layouts: 69.6 us -> 55.7 us
    dot_general x40, matrix products: 62.3 us -> 37.9 us  [one_one_block(): jnp.dot(shares, single_value, preferred_element_type=jnp.float32)]
    all_to_all x2 -> x0, local copies, waits for them, and re-layouts: 11.5 us -> none  [on_device(): lax.all_to_all(result, 'rows', split_axis=0, concat_axis=1, tiled=True)]
    unnamed x27 -> x43, local copies, waits for them, and re-layouts: 36.2 us -> 33.2 us
  transfers between devices with their start and end apart: 4 -> 4, of which waited for: 2 -> 2; matrix products, arithmetic and copies ran while one was open for 7% -> 8% of each run, Pallas kernels for 0% -> 0%
where the time goes in v1:
time: 288 us; the launch traced here: 282 us
  matrix products  89.1 us (31%)
  blocking collectives  83.7 us (29%)
  local copies, waits for them, and re-layouts  55.7 us (19%)
  other arithmetic  18 us (6%)
  waiting for transfers between devices  16.6 us (6%)
  starting transfers between devices  16.1 us (6%)
    dot_general x40, matrix products, one_one_block(): jnp.dot(block_query, single_key.T, preferred_element_type=jnp.float32)  41.5 us
    dot_general x40, matrix products, one_one_block(): jnp.dot(shares, single_value, preferred_element_type=jnp.float32)  37.9 us
    unnamed x43, local copies, waits for them, and re-layouts  33.2 us
    all_to_all x1, blocking collectives, trade_parts(): received = lax.all_to_all(jnp.stack(cells), mesh_axis, 0, 0)  24 us
    psum x1, blocking collectives, on_device(): lax.psum((table_hot[:, None] * first_local[None, :], table_hot * count_lo...  23.4 us
    psum x1, blocking collectives, on_device(): second_sum = lax.psum(table_hot[:, None] * second_local[None, :], 'rows')  17.1 us
    all_to_all x1, waiting for transfers between devices, on_device(): lax.all_to_all(normed, 'feat', split_axis=0, concat_axis=1, tiled=True)  11 us
    all_gather x1, blocking collectives, on_device(): every_value = lax.all_gather(local_value, 'feat', axis=0, tiled=True)  10.2 us
  transfers between devices with their start and end apart: 4, of which 2 were waited for; matrix products, arithmetic and copies ran while one was open for 8% of the time, Pallas kernels for 0%

profile of v1, /device:TPU:0, one launch (start us, length us, event | category | flops | bytes accessed | tf_op | source)
XLA Modules:
  0.0 282.1 jit_solution(13969307917819574657)
XLA Ops:
  0.0 1.3 dynamic_slice.44
  3.0 1.4 fusion.65
  5.6 1.6 fusion.40
  7.2 23.4 %all-reduce = (f32[8,20]{1,0:T(8,128)S(1)}, f32[8]{0:T(128)S(1)}) all-reduce(f32[8,20]{1,0:T(8,128)S(1)} %broadcast_multiply_fusion.1, f32[8]{0:T(128)S(1)} %compare_select_fusion.2), channel_id=1, replica_groups=mesh['rows'=8,'feat'=4] {'rows'}, use_global_device_ids=true, to_apply=%region_1.2 | all-reduce | flops 168 | bytes 1344 | tf_op jit(solution)/shard_map/psum | solution.py:81
  31.3 1.7 fusion.38
  33.0 17.1 %psum.23 = f32[8,20]{1,0:T(8,128)S(1)} all-reduce(f32[8,20]{1,0:T(8,128)S(1)} %broadcast_multiply_fusion), channel_id=1, replica_groups=mesh['rows'=8,'feat'=4] {'rows'}, use_global_device_ids=true, to_apply=%region_5.6 | all-reduce | flops 160 | bytes 1280 | tf_op jit(solution)/shard_map/psum | solution.py:88
  50.2 2.5 fusion.39
  52.7 3.5 %all-to-all-start = ((bf16[128,20,128]{2,1,0:T(8,128)(2,1)}), bf16[128,20,128]{2,1,0:T(8,128)(2,1)S(1)}, u32[]{:S(2)}, u32[]{:S(2)}) async-start(bf16[128,20,128]{2,1,0:T(8,128)(2,1)} %fusion.39), calls=%async_computation | async-start | bytes 1572864 | tf_op jit(solution)/shard_map/all_to_all | solution.py:92
  56.8 11.0 %all-to-all-done = bf16[128,20,128]{2,1,0:T(8,128)(2,1)S(1)} async-done(((bf16[128,20,128]{2,1,0:T(8,128)(2,1)}), bf16[128,20,128]{2,1,0:T(8,128)(2,1)S(1)}, u32[]{:S(2)}, u32[]{:S(2)}) %all-to-all-start) | async-done | bytes 655392 | tf_op jit(solution)/shard_map/all_to_all | solution.py:92
  68.9 1.3 copy.105
  71.5 10.6 %while.25 = (s32[]{:T(128)}, bf16[2,16,80,4,32]{2,4,3,1,0:T(8,128)(2,1)}, bf16[2,16,80,4,32]{2,4,3,1,0:T(8,128)(2,1)}, bf16[2,16,80,4,32]{2,4,3,1,0:T(8,128)(2,1...) while((s32[]{:T(128)}, bf16[2,16,80,4,32]{2,4,3,1,0:T(8,128)(2,1)}, ...), condition=%wide.region_9.10_spmd, body=%wide.region_6.9_spmd.sunk | while | flops 55050320 | bytes 12310625 | solution.py:55
  72.1 3.4 %fusion.87 = (f32[16,4,80]{2,1,0:T(4,128)S(1)}, f32[16,4,80,80]{2,3,1,0:T(8,128)S(1)}) fusion(f32[16,4,80,80]{2,3,1,0:T(8,128)S(1)} %fusion.86), kind=kOutput, calls=%fused_computation.105.clone.1 | output fusion | flops 1638479 | bytes 3297280 | tf_op jit(solution)/shard_map/while/body/eval_jaxpr/sub | solution.py:47
  75.6 1.3 fusion.88
  77.4 3.4 %fusion.87 = (f32[16,4,80]{2,1,0:T(4,128)S(1)}, f32[16,4,80,80]{2,3,1,0:T(8,128)S(1)}) fusion(f32[16,4,80,80]{2,3,1,0:T(8,128)S(1)} %fusion.86), kind=kOutput, calls=%fused_computation.105.clone.1 | output fusion | flops 1638479 | bytes 3297280 | tf_op jit(solution)/shard_map/while/body/eval_jaxpr/sub | solution.py:47
  80.8 1.3 fusion.88
  82.1 1.7 fusion.41
  86.1 3.4 %all-to-all-start.2 = ((bf16[8,2,2560]{2,1,0:T(2,128)(2,1)}), bf16[8,2,2560]{2,1,0:T(2,128)(2,1)S(1)}, u32[]{:S(2)}, u32[]{:S(2)}) async-start(bf16[8,2,2560]{2,1,0:T(2,128)(2,1)} %reshape.229), calls=%async_computation.2 | async-start | bytes 163840 | tf_op jit(solution)/shard_map/all_to_all | solution.py:132
  90.8 5.6 %all-to-all-done.2 = bf16[8,2,2560]{2,1,0:T(2,128)(2,1)S(1)} async-done(((bf16[8,2,2560]{2,1,0:T(2,128)(2,1)}), bf16[8,2,2560]{2,1,0:T(2,128)(2,1)S(1)}, u32[]{:S(2)}, u32[]{:S(2)}) %all-to-all-start.2) | async-done | bytes 81952 | tf_op jit(solution)/shard_map/all_to_all | solution.py:132
  96.4 3.4 %all-to-all-start.3 = ((bf16[8,2,2560]{2,1,0:T(2,128)(2,1)}), bf16[8,2,2560]{2,1,0:T(2,128)(2,1)S(1)}, u32[]{:S(2)}, u32[]{:S(2)}) async-start(bf16[8,2,2560]{2,1,0:T(2,128)(2,1)} %reshape.231), calls=%async_computation.3 | async-start | bytes 163840 | tf_op jit(solution)/shard_map/all_to_all | solution.py:133
  99.8 1.2 convolution_convert_fusion.2
  100.9 3.1 %reshape.208 = bf16[32,8,40,32]{3,2,1,0:T(8,128)(2,1)S(1)} reshape(bf16[32,80,128]{2,1,0:T(8,128)(2,1)} %convolution_convert_fusion.2) | data formatting | bytes 1310720 | tf_op jit(solution)/shard_map/reshape | solution.py:109
  104.0 2.5 copy.109
  106.5 5.8 %reshape.227 = bf16[8,2,20480]{2,1,0:T(2,128)(2,1)} reshape(bf16[8,32,32,40]{3,2,1,0:T(8,128)(2,1)} %bitcast.184) | data formatting | bytes 1310720
  112.9 5.9 %all-to-all-start.1 = ((bf16[8,2,20480]{2,1,0:T(2,128)(2,1)}), bf16[8,2,20480]{2,1,0:T(2,128)(2,1)S(1)}, u32[]{:S(2)}, u32[]{:S(2)}) async-start(bf16[8,2,20480]{2,1,0:T(2,128)(2,1)} %reshape.227), calls=%async_computation.1 | async-start | bytes 1310720 | tf_op jit(solution)/shard_map/all_to_all | solution.py:131
  120.1 9.1 %all_gather.6 = bf16[128,1,40,32]{2,3,1,0:T(8,128)(2,1)S(1)} all-gather(bf16[32,1,40,32]{2,3,1,0:T(8,128)(2,1)S(1)} %bitcast.192), channel_id=1, replica_groups=mesh['rows'=8,'feat'=4] {'feat'}, dimensions={0}, use_global_device_ids=true | all-gather | bytes 409600 | tf_op jit(solution)/shard_map/all_gather | solution.py:134
  129.2 2.9 %copy.116 = bf16[40,128,32]{2,1,0:T(8,128)(2,1)} copy(bf16[40,128,32]{0,2,1:T(8,128)(2,1)S(1)} %bitcast.188) | data formatting | bytes 655360
  132.5 10.2 %all_gather.7 = bf16[128,1,40,32]{2,3,1,0:T(8,128)(2,1)S(1)} all-gather(bf16[32,1,40,32]{2,3,1,0:T(8,128)(2,1)S(1)} %bitcast.193), channel_id=1, replica_groups=mesh['rows'=8,'feat'=4] {'feat'}, dimensions={0}, use_global_device_ids=true | all-gather | bytes 409600 | tf_op jit(solution)/shard_map/all_gather | solution.py:135
  142.7 2.9 %copy.117 = bf16[40,128,32]{2,1,0:T(8,128)(2,1)} copy(bf16[40,128,32]{0,2,1:T(8,128)(2,1)S(1)} %bitcast.189) | data formatting | bytes 655360
  145.5 3.3 %reshape.228 = bf16[8,32,32,40]{3,2,1,0:T(8,128)(2,1)S(1)} reshape(bf16[8,2,20480]{2,1,0:T(2,128)(2,1)S(1)} %all-to-all-done.1) | data formatting | bytes 1310720
  148.9 4.9 %copy.115 = bf16[40,256,32]{2,1,0:T(8,128)(2,1)} copy(bf16[40,256,32]{0,2,1:T(8,128)(2,1)S(1)} %bitcast.185) | data formatting | bytes 1310720
  153.8 81.5 %while.26 = (s32[]{:T(128)}, bf16[40,256,32]{1,2,0:T(8,128)(2,1)S(1)}, bf16[40,256,32]{2,1,0:T(8,128)(2,1)}, bf16[40,128,32]{2,1,0:T(8,128)(2,1)}, bf16[40,128,3...) while((s32[]{:T(128)}, ...), condition=%wide.region_16.17_spmd.clone, body=%wide.region_13.16_spmd.clone.sunk | while | flops 4529666 | bytes 549597 | solution.py:161
  155.8 1.0 fusion.90
  157.8 1.0 fusion.90
  164.0 1.0 fusion.90
  172.1 1.0 fusion.90
  180.3 1.0 fusion.90
  186.4 1.0 fusion.90
  188.4 1.0 fusion.90
  194.5 1.0 fusion.90
  235.3 3.5 %copy.118 = bf16[40,256,32]{0,2,1:T(8,128)(2,1)S(1)} copy(bf16[40,256,32]{1,2,0:T(8,128)(2,1)S(1)} %get-tuple-element.83) | data formatting | bytes 1310720 | tf_op jit(solution)/shard_map/while | solution.py:161
  239.1 1.3 copy-done.1
  240.5 5.0 %reshape.233 = bf16[8,2,20480]{2,1,0:T(2,128)(2,1)S(1)} reshape(bf16[8,32,1,32,40]{4,3,2,1,0:T(8,128)(2,1)} %bitcast.191) | data formatting | bytes 1310720
  245.5 24.0 %all_to_all.74 = bf16[8,2,20480]{2,1,0:T(2,128)(2,1)S(1)} all-to-all(bf16[8,2,20480]{2,1,0:T(2,128)(2,1)S(1)} %reshape.233), channel_id=1, replica_groups=mesh['rows'=8,'feat'=4] {'rows'}, dimensions={0} | all-to-all | bytes 1310720 | tf_op jit(solution)/shard_map/all_to_all | solution.py:16
  269.5 3.3 %reshape.234 = bf16[8,32,1,32,40]{4,3,2,1,0:T(8,128)(2,1)S(1)} reshape(bf16[8,2,20480]{2,1,0:T(2,128)(2,1)S(1)} %all_to_all.74) | data formatting | bytes 1310720
  272.8 1.8 bitcast_bitcast_fusion
  274.6 3.2 %copy.126 = bf16[32,8,1,40,32]{4,3,1,0,2:T(8,128)(2,1)S(1)} copy(bf16[32,8,1,40,32]{3,4,2,0,1:T(8,128)(2,1)} %bitcast_bitcast_fusion) | data formatting | bytes 1310720 | tf_op jit(solution)/shard_map/reshape | solution.py:17
  277.8 2.1 reshape_reshape.15
  279.9 2.2 fusion.42
  (195 shorter events, 84.8 us)
Async XLA Ops:
  0.0 67.9 %copy-start = (bf16[128,384]{1,0:T(8,128)(2,1)S(1)}, bf16[128,384]{1,0:T(8,128)(2,1)}, u32[]{:S(2)}) copy-start(bf16[128,384]{1,0:T(8,128)(2,1)} %param.16) | copy-start | bytes 294916
  5.5 50.6 %copy-start.11 = (s32[1024]{0:T(1024)S(1)}, s32[1024]{0:T(1024)}, u32[]{:S(2)}) copy-start(s32[1024]{0:T(1024)} %param.15) | copy-start | bytes 12292
  52.7 15.1 %all-to-all-start = ((bf16[128,20,128]{2,1,0:T(8,128)(2,1)}), bf16[128,20,128]{2,1,0:T(8,128)(2,1)S(1)}, u32[]{:S(2)}, u32[]{:S(2)}) async-start(bf16[128,20,128]{2,1,0:T(8,128)(2,1)} %fusion.39), calls=%async_computation | async-start | bytes 1572864 | tf_op jit(solution)/shard_map/all_to_all | solution.py:92
  71.5 10.6 %copy-start.9 = (bf16[128,128]{1,0:T(8,128)(2,1)S(1)}, bf16[128,128]{1,0:T(8,128)(2,1)}, u32[]{:S(2)}) copy-start(bf16[128,128]{1,0:T(8,128)(2,1)} %param.17) | copy-start | bytes 98308
  72.1 3.4 %copy-start.2 = (bf16[2,16,80,4,32]{2,4,3,1,0:T(8,128)(2,1)S(1)}, bf16[2,16,80,4,32]{2,4,3,1,0:T(8,128)(2,1)}, u32[]{:S(2)}) copy-start(bf16[2,16,80,4,32]{2,4,3,1,0:T(8,128)(2,1)} %get-tuple-element.283) | copy-start | bytes 1966084 | tf_op jit(solution)/shard_map/while
  77.4 3.4 %copy-start.2 = (bf16[2,16,80,4,32]{2,4,3,1,0:T(8,128)(2,1)S(1)}, bf16[2,16,80,4,32]{2,4,3,1,0:T(8,128)(2,1)}, u32[]{:S(2)}) copy-start(bf16[2,16,80,4,32]{2,4,3,1,0:T(8,128)(2,1)} %get-tuple-element.283) | copy-start | bytes 1966084 | tf_op jit(solution)/shard_map/while
  82.1 2.3 copy-start.8
  86.1 10.3 %all-to-all-start.2 = ((bf16[8,2,2560]{2,1,0:T(2,128)(2,1)}), bf16[8,2,2560]{2,1,0:T(2,128)(2,1)S(1)}, u32[]{:S(2)}, u32[]{:S(2)}) async-start(bf16[8,2,2560]{2,1,0:T(2,128)(2,1)} %reshape.229), calls=%async_computation.2 | async-start | bytes 163840 | tf_op jit(solution)/shard_map/all_to_all | solution.py:132
  96.4 3.4 %copy-start.4 = (bf16[8,2,2560]{2,1,0:T(2,128)(2,1)}, bf16[8,2,2560]{2,1,0:T(2,128)(2,1)S(1)}, u32[]{:S(2)}) copy-start(bf16[8,2,2560]{2,1,0:T(2,128)(2,1)S(1)} %all-to-all-done.2) | copy-start | bytes 245764
  96.4 15.8 %all-to-all-start.3 = ((bf16[8,2,2560]{2,1,0:T(2,128)(2,1)}), bf16[8,2,2560]{2,1,0:T(2,128)(2,1)S(1)}, u32[]{:S(2)}, u32[]{:S(2)}) async-start(bf16[8,2,2560]{2,1,0:T(2,128)(2,1)} %reshape.231), calls=%async_computation.3 | async-start | bytes 163840 | tf_op jit(solution)/shard_map/all_to_all | solution.py:133
  106.5 12.9 %copy-start.12 = (s32[8]{0:T(128)S(1)}, s32[8]{0:T(128)}, u32[]{:S(2)}) copy-start(s32[8]{0:T(128)} %param.13) | copy-start | bytes 100
  106.5 13.2 %copy-start.5 = (bf16[8,2,2560]{2,1,0:T(2,128)(2,1)S(1)}, bf16[8,2,2560]{2,1,0:T(2,128)(2,1)}, u32[]{:S(2)}) copy-start(bf16[8,2,2560]{2,1,0:T(2,128)(2,1)} %copy-done.4) | copy-start | bytes 245764
  112.2 0.6 copy-start.6
  112.9 32.7 %all-to-all-start.1 = ((bf16[8,2,20480]{2,1,0:T(2,128)(2,1)}), bf16[8,2,20480]{2,1,0:T(2,128)(2,1)S(1)}, u32[]{:S(2)}, u32[]{:S(2)}) async-start(bf16[8,2,20480]{2,1,0:T(2,128)(2,1)} %reshape.227), calls=%async_computation.1 | async-start | bytes 1310720 | tf_op jit(solution)/shard_map/all_to_all | solution.py:131
  118.8 13.3 %copy-start.7 = (bf16[8,2,2560]{2,1,0:T(2,128)(2,1)S(1)}, bf16[8,2,2560]{2,1,0:T(2,128)(2,1)}, u32[]{:S(2)}) copy-start(bf16[8,2,2560]{2,1,0:T(2,128)(2,1)} %copy-done.6) | copy-start | bytes 245764
  148.9 4.9 %copy-start.3 = (bf16[40,256,32]{1,2,0:T(8,128)(2,1)S(1)}, bf16[40,256,32]{1,2,0:T(8,128)(2,1)}, u32[]{:S(2)}) copy-start(bf16[40,256,32]{1,2,0:T(8,128)(2,1)} %custom-call.4) | copy-start | bytes 1966084
  239.1 1.4 copy-start.1
  277.8 2.1 copy-start.10
